TPU v7x, 32 devices: a whole 2x2x4 slice. The times are simulated.
32 devices in a mesh: grp: 2 (over x), az: 8 (over z, y), ax: 2 (over core).
Axes of the slice: x: 2, y: 2, z: 4, core: 2. Of those that a mesh axis runs over, the one named last changes fastest.
Arguments:
- cavity_block: float32 [8, 96, 32, 256], P(None, 'grp', 'az', 'ax'), may hold values from -95 to 95
- shell_block: float32 [8, 6, 32, 256], P(None, None, 'az', 'ax'), may hold values from -95 to 95
- column_matrix: float32 [2, 48, 48], P('grp'), may hold values from -2 to 6, as said below
- shell_matrix: float32 [6, 6], replicated, may hold values from -2 to 6, as said below
- shifted_diagonal: float32 [96, 32, 256], P('grp', 'az', 'ax'), may hold values from 1.6 to 3
- shell_diagonal: float32 [6, 32, 256], P(None, 'az', 'ax'), may hold values from 1.6 to 3
- wet_area: float32 [32, 256], P('az', 'ax'), may hold values from 0.3 to 1.5
Outputs:
- cavity_solution: float32 [8, 96, 32, 256], P(None, 'grp', 'az', 'ax')
- cavity_residual: float32 [8, 96, 32, 256], P(None, 'grp', 'az', 'ax')
- shell_solution: float32 [8, 6, 32, 256], P(None, None, 'az', 'ax')
- shell_residual: float32 [8, 6, 32, 256], P(None, None, 'az', 'ax')
Inputs may be any that keep to these rules, and one draw needn't show every extreme that they name: `column_matrix`: each symmetric and positive definite. `shell_matrix`: symmetric and positive definite.
All inputs are finite; a program needn't handle non-finite values.
Results may differ from a plain program's by a relative error of at most 0.0015.
Values sent between devices are 32-bit elements; how exact they have to be, the bound alone decides.
No kernel may reach another device: no remote copies, remote signals or barrier semaphores. Data moves between devices by JAX's collectives and lax.ppermute only.
A program may use at most 128 MiB of HBM per device.

v0:
```python
import jax
import jax.numpy as jnp
from jax import lax
from jax.sharding import PartitionSpec as P

ITERS = 3
exact_mode = lax.Precision.HIGHEST


def swapped(block, axis, apart):
    count = lax.axis_size(axis)
    route = []
    for low in range(count):
        high = low | 1 << apart
        if high != low and high < count:
            route += [(low, high), (high, low)]
    return lax.ppermute(block, axis, route)


def extended(array, sides, width, wrap):
    for axis, dim in sides:
        peers, length = (lax.axis_size(axis), array.shape[dim])
        up = [(i, (i + 1) % peers) for i in range(peers if wrap else peers - 1)]
        down = [(j, i) for i, j in up]
        last = lax.slice_in_dim(array, length - width, length, axis=dim)
        first = lax.slice_in_dim(array, 0, width, axis=dim)
        before = lax.ppermute(last, axis, up)
        after = lax.ppermute(first, axis, down)
        array = jnp.concatenate([before, array, after], axis=dim)
    return array


def solve_posdef(gram_matrix, targets):
    factor = jnp.linalg.cholesky(gram_matrix)
    middle = lax.linalg.triangular_solve(factor, targets, left_side=True, lower=True)
    return lax.linalg.triangular_solve(factor, middle, left_side=True, lower=True, transpose_a=True)


def products(first_set, second_set):
    return jnp.einsum("vrax,wrax->vw", first_set, second_set, precision=exact_mode)


def combine(vector_set, mixing):
    return jnp.einsum("vrax,vw->wrax", vector_set, mixing, precision=exact_mode)


def column_part(vector_set, matrix):
    flat_set = vector_set.reshape(vector_set.shape[0], vector_set.shape[1], -1)
    mixed_set = jnp.einsum("rs,vsc->vrc", matrix, flat_set, precision=exact_mode)
    return mixed_set.reshape(vector_set.shape)


def coupled(result, vector_set, wet_area, layout):
    half, interface_row, outer_flag = layout
    iface_own = lax.dynamic_slice_in_dim(vector_set, interface_row, 1, 1)
    wall_own = vector_set[:, half - 1 : half]
    sent = jnp.concatenate([iface_own, wall_own], axis=1)
    received = swapped(sent, "grp", 0)
    result_row = lax.dynamic_slice_in_dim(result, interface_row, 1, 1)
    result = lax.dynamic_update_slice_in_dim(
        result, result_row - received[:, 0:1], interface_row, 1
    )
    wall = outer_flag * wall_own + (1.0 - outer_flag) * received[:, 1:2]
    shell_top = vector_set[:, half : half + 1]
    result = result.at[:, half - 1 : half].add(-outer_flag * wet_area * shell_top)
    result = result.at[:, half : half + 1].add(-wet_area * wall)
    return result


def apply_shallow(vector_set, matrix, diagonal_set, wet_area, layout):
    beside_all = extended(vector_set, (("az", 2),), 1, True)
    along = extended(vector_set, (("ax", 3),), 1, False)
    neighbours = beside_all[:, :, 2:] + beside_all[:, :, :-2] + along[..., 2:] + along[..., :-2]
    result = column_part(vector_set, matrix) + (4.0 + diagonal_set) * vector_set - neighbours
    return coupled(result, vector_set, wet_area, layout)


def per_device(
    cavity_block,
    shell_block,
    column_matrix,
    shell_matrix,
    shifted_diagonal,
    shell_diagonal,
    wet_area,
):
    group_index = lax.axis_index("grp")
    outer_flag = (group_index == 1).astype(jnp.float32)
    shell_share = 1.0 - outer_flag
    half = column_matrix.shape[1]
    shell_rows = shell_matrix.shape[0]
    interface_row = jnp.where(group_index == 1, 0, half - 1).astype(jnp.int32)
    layout = (half, interface_row, outer_flag)
    upper = jnp.concatenate([column_matrix[0], jnp.zeros((half, shell_rows), jnp.float32)], axis=1)
    lower = jnp.concatenate([jnp.zeros((shell_rows, half), jnp.float32), shell_matrix], axis=1)
    matrix = jnp.concatenate([upper, lower], axis=0)
    right_side = jnp.concatenate([cavity_block, shell_block], axis=1)
    diagonal_own = jnp.concatenate([shifted_diagonal, shell_diagonal], axis=0)

    def moments_local(first_set, second_set):
        cavity_part = products(first_set[:, :half], second_set[:, :half])
        return cavity_part + shell_share * products(first_set[:, half:], second_set[:, half:])

    residual = right_side
    direction = right_side
    solution = jnp.zeros_like(right_side)
    start_core = residual
    norms_now = lax.psum(moments_local(start_core, start_core), ("grp", "az", "ax"))
    for sweep in range(ITERS):
        image_set = apply_shallow(direction, matrix, diagonal_own, wet_area, layout)
        direction_core = direction
        residual_core = residual
        curvature, crossing, squares = lax.psum(
            (
                moments_local(direction_core, image_set),
                moments_local(image_set, residual_core),
                moments_local(image_set, image_set),
            ),
            ("grp", "az", "ax"),
        )
        step_mix = solve_posdef(curvature, norms_now)
        norms_next = norms_now - jnp.dot(step_mix.T, crossing, precision=exact_mode)
        norms_next = norms_next - jnp.dot(crossing.T, step_mix, precision=exact_mode)
        norms_next = norms_next + jnp.dot(
            jnp.dot(step_mix.T, squares, precision=exact_mode), step_mix, precision=exact_mode
        )
        solution = solution + combine(direction_core, step_mix)
        residual = residual - combine(image_set, step_mix)
        if sweep + 1 < ITERS:
            turn_mix = solve_posdef(norms_now, norms_next)
            direction = residual + combine(direction, turn_mix)
            norms_now = norms_next
    return (solution[:, :half], residual[:, :half], solution[:, half:], residual[:, half:])


def solution(mesh):
    return jax.shard_map(
        per_device,
        mesh=mesh,
        in_specs=(
            P(None, "grp", "az", "ax"),
            P(None, None, "az", "ax"),
            P("grp", None, None),
            P(),
            P("grp", "az", "ax"),
            P(None, "az", "ax"),
            P("az", "ax"),
        ),
        out_specs=(
            P(None, "grp", "az", "ax"),
            P(None, "grp", "az", "ax"),
            P(None, None, "az", "ax"),
            P(None, None, "az", "ax"),
        ),
        check_vma=False,
    )
```

profile of v0, /device:TPU:0, one launch (start us, length us, event | category | flops | bytes accessed | tf_op | source)
XLA Modules:
  0.0 250.7 jit_solution(17498085943303923312)
XLA Ops:
  0.6 2.5 fusion.124
  5.1 2.4 collective-permute-start.3
  7.9 1.3 collective-permute-start.2
  10.0 2.3 collective-permute-start.1
  12.3 3.0 %collective-permute-start = (f32[8,54,1,128]{3,0,1,2:T(8,128)}, f32[8,54,1,128]{3,0,1,2:T(8,128)}, u32[]{:S(2)}, u32[]{:S(2)}) collective-permute-start(f32[8,54,1,128]{3,0,1,2:T(8,128)} %get-tuple-element.110), channel_id=1, source_target_pairs={{2,0},{4,2},{6,4},{8,6},{10,8},{12,10},{14,12},{0,14},{3,1},{5,3},... | collective-permute-start | bytes 663560 | tf_op jit(solution)/shard_map/ppermute | solution.py:28
  16.7 1.7 collective-permute-start.4
  18.4 1.9 convolution_bitcast_fusion.3
  21.4 2.4 convolution_bitcast_fusion.2
  24.9 1.4 copy.165
  26.3 2.5 fusion.26
  31.0 1.9 convolution_bitcast_fusion.15
  32.9 1.8 convolution_bitcast_fusion.13
  35.7 38.6 %all-reduce.3 = (f32[8,8]{0,1:T(8,128)S(1)}, f32[8,8]{1,0:T(8,128)S(1)}, f32[8,8]{0,1:T(8,128)S(1)}, f32[8,8]{0,1:T(8,128)S(1)}) all-reduce(f32[8,8]{0,1:T(8,128)S(1)} %copy-done.18, f32[8,8]{1,0:T(8,128)S(1)} %bitcast.241, f32[8,8]{0,1:T(8,128)S(1)} %fusion.11, ...), channel_id=1, replica_groups=mesh['grp'=2,'az'=8,'ax'=2] {'grp','az','ax'}, use_global_device_ids=true, to_apply=%region_3.0 | all-reduce | flops 256 | bytes 2048 | tf_op jit(solution)/shard_map/psum | solution.py:108
  77.5 1.9 fusion.31
  85.0 1.2 fusion.121
  88.4 2.1 copy.206
  90.6 1.9 collective-permute-start.8
  93.4 1.3 collective-permute-start.7
  94.7 2.4 collective-permute-start.6
  97.1 2.4 collective-permute-start.5
  99.5 3.1 %convolution_bitcast_fusion.1 = f32[8,54,512]{2,1,0:T(8,128)} fusion(f32[8,54,512]{2,0,1:T(8,128)S(1)} %bitcast.235, f32[6,6]{1,0:T(8,128)S(1)} %copy-done.14, f32[48,48]{1,0:T(8,128)} %bitcast.238), kind=kOutput, calls=%fused_computation.1 | convolution fusion | flops 143341808 | bytes 1778832 | tf_op jit(solution)/shard_map/rs,vsc->vrc/dot_general | solution.py:49
  103.3 2.3 collective-permute-start.9
  107.6 1.2 custom-call.23
  108.9 1.1 copy.207
  110.0 1.3 copy.205
  112.0 2.5 fusion.22
  116.0 1.8 convolution_bitcast_fusion.11
  117.8 1.8 convolution_bitcast_fusion.9
  119.6 1.8 convolution_bitcast_fusion.7
  122.3 37.7 %all-reduce.2 = (f32[8,8]{0,1:T(8,128)S(1)}, f32[8,8]{0,1:T(8,128)}, f32[8,8]{0,1:T(8,128)}) all-reduce(f32[8,8]{0,1:T(8,128)S(1)} %fusion.7, f32[8,8]{0,1:T(8,128)S(1)} %fusion.5, f32[8,8]{0,1:T(8,128)S(1)} %fusion.3), channel_id=1, replica_groups=mesh['grp'=2,'az'=8,'ax'=2] {'grp','az','ax'}, use_global_device_ids=true, to_apply=%region_6.10 | all-reduce | flops 192 | bytes 1536 | tf_op jit(solution)/shard_map/psum | solution.py:113
  166.8 1.5 fusion.119
  170.3 1.9 convolution_add_fusion.2
  172.1 2.2 copy.237
  174.4 2.0 collective-permute-start.13
  177.3 1.3 collective-permute-start.12
  178.6 2.7 %collective-permute-start.11 = (f32[8,54,1,128]{3,0,1,2:T(8,128)}, f32[8,54,1,128]{3,0,1,2:T(8,128)S(1)}, u32[]{:S(2)}, u32[]{:S(2)}) collective-permute-start(f32[8,54,1,128]{3,0,1,2:T(8,128)} %get-tuple-element.101), channel_id=1, source_target_pairs={{0,2},{2,4},{4,6},{6,8},{8,10},{10,12},{12,14},{14,0},{1,3},{3,5},... | collective-permute-start | bytes 663560 | tf_op jit(solution)/shard_map/ppermute | solution.py:27
  181.3 2.1 collective-permute-start.10
  183.4 3.1 %convolution_bitcast_fusion = f32[8,54,512]{2,1,0:T(8,128)} fusion(f32[8,54,512]{2,0,1:T(8,128)S(1)} %bitcast.236, f32[6,6]{1,0:T(8,128)S(1)} %copy-done.14, f32[48,48]{1,0:T(8,128)} %bitcast.239), kind=kOutput, calls=%fused_computation | convolution fusion | flops 143341808 | bytes 1778832 | tf_op jit(solution)/shard_map/rs,vsc->vrc/dot_general | solution.py:49
  187.1 2.2 collective-permute-start.14
  189.3 1.1 copy.238
  190.5 1.3 copy.236
  192.7 1.8 collective-permute-done.10
  194.5 2.4 fusion.18
  198.5 1.8 convolution_bitcast_fusion.5
  200.5 38.7 %psum.63 = f32[8,8]{0,1:T(8,128)S(1)} all-reduce(f32[8,8]{0,1:T(8,128)S(1)} %fusion.1), channel_id=1, replica_groups=mesh['grp'=2,'az'=8,'ax'=2] {'grp','az','ax'}, use_global_device_ids=true, to_apply=%region_9.13 | all-reduce | flops 64 | bytes 512 | tf_op jit(solution)/shard_map/psum | solution.py:113
  245.4 1.1 slice-done.2
  246.6 1.1 copy.249
  247.8 1.4 copy.250
  (165 shorter events, 48.5 us)
Async XLA Ops:
  0.6 2.5 %copy-start.6 = (f32[8,6,4,128]{3,2,1,0:T(4,128)S(1)}, f32[8,6,4,128]{3,2,1,0:T(4,128)}, u32[]{:S(2)}) copy-start(f32[8,6,4,128]{3,2,1,0:T(4,128)} %param.25) | copy-start | bytes 294916
  5.1 19.4 %collective-permute-start.3 = (f32[8,54,4,1]{1,0,3,2:T(8,128)}, f32[8,54,4,1]{1,0,3,2:T(8,128)S(1)}, u32[]{:S(2)}, u32[]{:S(2)}) collective-permute-start(f32[8,54,4,1]{1,0,3,2:T(8,128)} %copy.166), channel_id=1, source_target_pairs={{0,1},{2,3},{4,5},{6,7},{8,9},{10,11},{12,13},{14,15},{16,17},{18,... | collective-permute-start | bytes 20744 | tf_op jit(solution)/shard_map/ppermute | solution.py:27
  7.5 10.9 %copy-start = (f32[8,48,4,128]{3,2,1,0:T(4,128)S(1)}, f32[8,48,4,128]{3,2,1,0:T(4,128)}, u32[]{:S(2)}) copy-start(f32[8,48,4,128]{3,2,1,0:T(4,128)} %param.24) | copy-start | bytes 2359300
  7.9 17.0 %collective-permute-start.2 = (f32[8,54,4,1]{1,0,3,2:T(8,128)S(1)}, f32[8,54,4,1]{1,0,3,2:T(8,128)S(1)}, u32[]{:S(2)}, u32[]{:S(2)}) collective-permute-start(f32[8,54,4,1]{1,0,3,2:T(8,128)S(1)} %copy.164), channel_id=1, source_target_pairs={{1,0},{3,2},{5,4},{7,6},{9,8},{11,10},{13,12},{15,14},{17,16},{19,... | collective-permute-start | bytes 20744 | tf_op jit(solution)/shard_map/ppermute | solution.py:28
  10.0 16.3 %collective-permute-start.1 = (f32[8,54,1,128]{3,0,1,2:T(8,128)}, f32[8,54,1,128]{3,0,1,2:T(8,128)}, u32[]{:S(2)}, u32[]{:S(2)}) collective-permute-start(f32[8,54,1,128]{3,0,1,2:T(8,128)} %get-tuple-element.111), channel_id=1, source_target_pairs={{0,2},{2,4},{4,6},{6,8},{8,10},{10,12},{12,14},{14,0},{1,3},{3,5},... | collective-permute-start | bytes 663560 | tf_op jit(solution)/shard_map/ppermute | solution.py:27
  12.3 14.0 %collective-permute-start = (f32[8,54,1,128]{3,0,1,2:T(8,128)}, f32[8,54,1,128]{3,0,1,2:T(8,128)}, u32[]{:S(2)}, u32[]{:S(2)}) collective-permute-start(f32[8,54,1,128]{3,0,1,2:T(8,128)} %get-tuple-element.110), channel_id=1, source_target_pairs={{2,0},{4,2},{6,4},{8,6},{10,8},{12,10},{14,12},{0,14},{3,1},{5,3},... | collective-permute-start | bytes 663560 | tf_op jit(solution)/shard_map/ppermute | solution.py:28
  16.7 12.1 %collective-permute-start.4 = (f32[8,2,4,128]{3,0,1,2:T(8,128)}, f32[8,2,4,128]{3,0,1,2:T(8,128)}, u32[]{:S(2)}, u32[]{:S(2)}) collective-permute-start(f32[8,2,4,128]{3,0,1,2:T(8,128)} %pad_maximum_fusion.12), channel_id=1, source_target_pairs={{0,16},{16,0},{1,17},{17,1},{2,18},{18,2},{3,19},{19,3},{4,20},{20... | collective-permute-start | bytes 98312 | tf_op jit(solution)/shard_map/ppermute | solution.py:17
  20.4 0.9 copy-start.8
  20.4 0.9 copy-start.14
  21.3 2.4 copy-start.21
  21.3 2.4 copy-start.11
  21.4 2.4 copy-start.19
  32.9 1.8 copy-start.7
  34.9 0.7 copy-start.18
  90.6 18.3 %collective-permute-start.8 = (f32[8,54,4,1]{1,0,3,2:T(8,128)}, f32[8,54,4,1]{1,0,3,2:T(8,128)}, u32[]{:S(2)}, u32[]{:S(2)}) collective-permute-start(f32[8,54,4,1]{1,0,3,2:T(8,128)} %copy.206), channel_id=1, source_target_pairs={{0,1},{2,3},{4,5},{6,7},{8,9},{10,11},{12,13},{14,15},{16,17},{18,... | collective-permute-start | bytes 20744 | tf_op jit(solution)/shard_map/ppermute | solution.py:27
  93.4 16.6 %collective-permute-start.7 = (f32[8,54,4,1]{1,0,3,2:T(8,128)}, f32[8,54,4,1]{1,0,3,2:T(8,128)S(1)}, u32[]{:S(2)}, u32[]{:S(2)}) collective-permute-start(f32[8,54,4,1]{1,0,3,2:T(8,128)} %copy.204), channel_id=1, source_target_pairs={{1,0},{3,2},{5,4},{7,6},{9,8},{11,10},{13,12},{15,14},{17,16},{19,... | collective-permute-start | bytes 20744 | tf_op jit(solution)/shard_map/ppermute | solution.py:28
  94.7 16.6 %collective-permute-start.6 = (f32[8,54,1,128]{3,0,1,2:T(8,128)}, f32[8,54,1,128]{3,0,1,2:T(8,128)S(1)}, u32[]{:S(2)}, u32[]{:S(2)}) collective-permute-start(f32[8,54,1,128]{3,0,1,2:T(8,128)} %get-tuple-element.107), channel_id=1, source_target_pairs={{0,2},{2,4},{4,6},{6,8},{8,10},{10,12},{12,14},{14,0},{1,3},{3,5},... | collective-permute-start | bytes 663560 | tf_op jit(solution)/shard_map/ppermute | solution.py:27
  97.1 14.9 %collective-permute-start.5 = (f32[8,54,1,128]{3,0,1,2:T(8,128)}, f32[8,54,1,128]{3,0,1,2:T(8,128)}, u32[]{:S(2)}, u32[]{:S(2)}) collective-permute-start(f32[8,54,1,128]{3,0,1,2:T(8,128)} %get-tuple-element.106), channel_id=1, source_target_pairs={{2,0},{4,2},{6,4},{8,6},{10,8},{12,10},{14,12},{0,14},{3,1},{5,3},... | collective-permute-start | bytes 663560 | tf_op jit(solution)/shard_map/ppermute | solution.py:28
  99.5 3.2 %copy-start.12 = (f32[8,1,4,128]{3,0,1,2:T(8,128)S(1)}, f32[8,1,4,128]{3,0,1,2:T(8,128)}, u32[]{:S(2)}) copy-start(f32[8,1,4,128]{3,0,1,2:T(8,128)} %get-tuple-element.104) | copy-start | bytes 49156
  99.5 3.2 %copy-start.13 = (f32[8,1,4,128]{3,0,1,2:T(8,128)S(1)}, f32[8,1,4,128]{3,0,1,2:T(8,128)}, u32[]{:S(2)}) copy-start(f32[8,1,4,128]{3,0,1,2:T(8,128)} %get-tuple-element.105) | copy-start | bytes 49156
  102.7 2.9 %copy-start.16 = (f32[8,8]{1,0:T(8,128)S(1)}, f32[8,8]{1,0:T(8,128)}, u32[]{:S(2)}) copy-start(f32[8,8]{1,0:T(8,128)} %copy.218) | copy-start | bytes 772
  103.3 11.2 %collective-permute-start.9 = (f32[8,2,4,128]{3,0,1,2:T(8,128)}, f32[8,2,4,128]{3,0,1,2:T(8,128)}, u32[]{:S(2)}, u32[]{:S(2)}) collective-permute-start(f32[8,2,4,128]{3,0,1,2:T(8,128)} %pad_maximum_fusion.13), channel_id=1, source_target_pairs={{0,16},{16,0},{1,17},{17,1},{2,18},{18,2},{3,19},{19,3},{4,20},{20... | collective-permute-start | bytes 98312 | tf_op jit(solution)/shard_map/ppermute | solution.py:17
  111.3 0.7 copy-start.9
  163.1 0.9 copy-start.17
  164.0 0.7 copy-start.20
  164.9 0.7 copy-start.15
  169.1 1.2 copy-start.2
  172.1 4.2 %copy-start.1 = (f32[8,54,4,1]{3,0,1,2:T(8,128)S(1)}, f32[8,54,4,1]{3,0,1,2:T(8,128)}, u32[]{:S(2)}) copy-start(f32[8,54,4,1]{3,0,1,2:T(8,128)} %get-tuple-element.102) | copy-start | bytes 20740
  174.4 15.0 %collective-permute-start.13 = (f32[8,54,4,1]{1,0,3,2:T(8,128)}, f32[8,54,4,1]{1,0,3,2:T(8,128)}, u32[]{:S(2)}, u32[]{:S(2)}) collective-permute-start(f32[8,54,4,1]{1,0,3,2:T(8,128)} %copy.237), channel_id=1, source_target_pairs={{0,1},{2,3},{4,5},{6,7},{8,9},{10,11},{12,13},{14,15},{16,17},{18,... | collective-permute-start | bytes 20744 | tf_op jit(solution)/shard_map/ppermute | solution.py:27
  177.3 13.2 %collective-permute-start.12 = (f32[8,54,4,1]{1,0,3,2:T(8,128)}, f32[8,54,4,1]{1,0,3,2:T(8,128)S(1)}, u32[]{:S(2)}, u32[]{:S(2)}) collective-permute-start(f32[8,54,4,1]{1,0,3,2:T(8,128)} %copy.235), channel_id=1, source_target_pairs={{1,0},{3,2},{5,4},{7,6},{9,8},{11,10},{13,12},{15,14},{17,16},{19,... | collective-permute-start | bytes 20744 | tf_op jit(solution)/shard_map/ppermute | solution.py:28
  178.6 13.4 %collective-permute-start.11 = (f32[8,54,1,128]{3,0,1,2:T(8,128)}, f32[8,54,1,128]{3,0,1,2:T(8,128)S(1)}, u32[]{:S(2)}, u32[]{:S(2)}) collective-permute-start(f32[8,54,1,128]{3,0,1,2:T(8,128)} %get-tuple-element.101), channel_id=1, source_target_pairs={{0,2},{2,4},{4,6},{6,8},{8,10},{10,12},{12,14},{14,0},{1,3},{3,5},... | collective-permute-start | bytes 663560 | tf_op jit(solution)/shard_map/ppermute | solution.py:27
  181.3 13.2 %collective-permute-start.10 = (f32[8,54,1,128]{3,0,1,2:T(8,128)}, f32[8,54,1,128]{3,0,1,2:T(8,128)}, u32[]{:S(2)}, u32[]{:S(2)}) collective-permute-start(f32[8,54,1,128]{3,0,1,2:T(8,128)} %get-tuple-element.100), channel_id=1, source_target_pairs={{2,0},{4,2},{6,4},{8,6},{10,8},{12,10},{14,12},{0,14},{3,1},{5,3},... | collective-permute-start | bytes 663560 | tf_op jit(solution)/shard_map/ppermute | solution.py:28
  187.1 9.8 %collective-permute-start.14 = (f32[8,2,4,128]{3,0,1,2:T(8,128)}, f32[8,2,4,128]{3,0,1,2:T(8,128)}, u32[]{:S(2)}, u32[]{:S(2)}) collective-permute-start(f32[8,2,4,128]{3,0,1,2:T(8,128)} %pad_maximum_fusion.14), channel_id=1, source_target_pairs={{0,16},{16,0},{1,17},{17,1},{2,18},{18,2},{3,19},{19,3},{4,20},{20... | collective-permute-start | bytes 98312 | tf_op jit(solution)/shard_map/ppermute | solution.py:17
  192.0 0.7 copy-start.10
  242.4 1.2 copy-start.5
  243.6 1.8 copy-start.3
  244.5 1.0 copy-start.4
  245.4 1.1 slice-start.2
  246.6 1.2 slice-start
  247.8 1.4 slice-start.3
  249.2 0.9 slice-start.1
where the time goes:
time: 252 us; the launch traced here: 251 us
  blocking collectives  115 us (46%)
  local copies, waits for them, and re-layouts  36.6 us (15%)
  matrix products  36.5 us (14%)
  starting transfers between devices  31.1 us (12%)
  other arithmetic  28.4 us (11%)
    psum x2, blocking collectives, per_device(): lax.psum((moments_local(direction_core, image_set), moments_local(image_s...  76.4 us
    psum x1, blocking collectives, per_device(): lax.psum(moments_local(start_core, start_core), ('grp', 'az', 'ax'))  38.6 us
    dot_general x14, matrix products, products(): jnp.einsum('vrax,wrax->vw', first_set, second_set, precision=exact_mode)  15.5 us
    ppermute x6, starting transfers between devices, extended(): before = lax.ppermute(last, axis, up)  13.6 us
    unnamed x50, local copies, waits for them, and re-layouts  12 us
    ppermute x6, starting transfers between devices, extended(): after = lax.ppermute(first, axis, down)  11.4 us
    dot_general x8, matrix products, combine(): return jnp.einsum('vrax,vw->wrax', vector_set, mixing, precision=exact_mode)  9.04 us
    dot_general x3, matrix products, column_part(): jnp.einsum('rs,vsc->vrc', matrix, flat_set, precision=exact_mode)  8.66 us
  transfers between devices with their start and end apart: 15, of which 2 were waited for; matrix products, arithmetic and copies ran while one was open for 14% of the time, Pallas kernels for 0%

commit v1 on v0

--- a/solution.py
+++ b/solution.py
@@ -105,7 +105,9 @@
     direction = right_side
     solution = jnp.zeros_like(right_side)
     start_core = residual
-    norms_now = lax.psum(moments_local(start_core, start_core), ("grp", "az", "ax"))
+    norms_now = jnp.sum(
+        lax.all_gather(moments_local(start_core, start_core), ("grp", "az", "ax")), axis=0
+    )
     for sweep in range(ITERS):
         image_set = apply_shallow(direction, matrix, diagonal_own, wet_area, layout)
         direction_core = direction

time: 252 us -> 291 us (1.15)
  blocking collectives: 115 us -> 153 us
    psum x1 -> x0, blocking collectives: 38.6 us -> none  [per_device(): lax.psum(moments_local(start_core, start_core), ('grp', 'az', 'ax'))]
    all_gather x0 -> x1, blocking collectives: none -> 38.5 us  [per_device(): lax.all_gather(moments_local(start_core, start_core), ('grp', 'az', 'ax'))]
    psum x2 -> x3, blocking collectives: 76.4 us -> 114 us  [per_device(): lax.psum((moments_local(direction_core, image_set), moments_local(image_s...]
    unnamed x50 -> x57, local copies, waits for them, and re-layouts: 12 us -> 12.9 us
  transfers between devices with their start and end apart: 15 -> 15, of which waited for: 2 -> 2; matrix products, arithmetic and copies ran while one was open for 14% -> 13% of each run, Pallas kernels for 0% -> 0%
where the time goes in v1:
time: 291 us; the launch traced here: 289 us
  blocking collectives  153 us (53%)
  local copies, waits for them, and re-layouts  37 us (13%)
  matrix products  35.8 us (12%)
  starting transfers between devices  31.2 us (11%)
  other arithmetic  29 us (10%)
    psum x3, blocking collectives, per_device(): lax.psum((moments_local(direction_core, image_set), moments_local(image_s...  114 us
    all_gather x1, blocking collectives, per_device(): lax.all_gather(moments_local(start_core, start_core), ('grp', 'az', 'ax'))  38.5 us
    dot_general x14, matrix products, products(): jnp.einsum('vrax,wrax->vw', first_set, second_set, precision=exact_mode)  14.9 us
    ppermute x6, starting transfers between devices, extended(): before = lax.ppermute(last, axis, up)  13.6 us
    unnamed x57, local copies, waits for them, and re-layouts  12.9 us
    ppermute x6, starting transfers between devices, extended(): after = lax.ppermute(first, axis, down)  11.5 us
    dot_general x8, matrix products, combine(): return jnp.einsum('vrax,vw->wrax', vector_set, mixing, precision=exact_mode)  9.04 us
    dot_general x3, matrix products, column_part(): jnp.einsum('rs,vsc->vrc', matrix, flat_set, precision=exact_mode)  8.67 us
  transfers between devices with their start and end apart: 15, of which 2 were waited for; matrix products, arithmetic and copies ran while one was open for 13% of the time, Pallas kernels for 0%

profile of v1, /device:TPU:0, one launch (start us, length us, event | category | flops | bytes accessed | tf_op | source)
XLA Modules:
  0.0 288.9 jit_solution(13106895905586489445)
XLA Ops:
  0.6 2.5 fusion.124
  5.1 2.4 collective-permute-start.3
  7.9 1.3 collective-permute-start.2
  9.2 2.4 collective-permute-start.1
  11.6 3.1 %collective-permute-start = (f32[8,54,1,128]{3,0,1,2:T(8,128)S(1)}, f32[8,54,1,128]{3,0,1,2:T(8,128)}, u32[]{:S(2)}, u32[]{:S(2)}) collective-permute-start(f32[8,54,1,128]{3,0,1,2:T(8,128)S(1)} %get-tuple-element.109), channel_id=1, source_target_pairs={{2,0},{4,2},{6,4},{8,6},{10,8},{12,10},{14,12},{0,14},{3,1},{5,3},... | collective-permute-start | bytes 663560 | tf_op jit(solution)/shard_map/ppermute | solution.py:28
  16.1 1.6 collective-permute-start.4
  17.7 1.9 convolution_bitcast_fusion.3
  20.0 38.5 %all-gather = f32[256,8]{1,0:T(8,128)S(1)} all-gather(f32[8,8]{1,0:T(8,128)S(1)} %copy.184), channel_id=2, replica_groups=mesh['grp'=2,'az'=8,'ax'=2] {'grp','az','ax'}, dimensions={0}, use_global_device_ids=true | all-gather | bytes 8448 | tf_op jit(solution)/shard_map/all_gather | solution.py:109
  60.9 2.4 convolution_bitcast_fusion.2
  64.0 1.2 custom-call.19
  65.2 1.4 copy.167
  66.6 1.3 copy.165
  68.6 2.3 fusion.26
  73.2 1.9 convolution_bitcast_fusion.15
  75.1 1.8 convolution_bitcast_fusion.13
  77.5 37.2 %all-reduce.3 = (f32[8,8]{1,0:T(8,128)S(1)}, f32[8,8]{0,1:T(8,128)S(1)}, f32[8,8]{0,1:T(8,128)S(1)}) all-reduce(f32[8,8]{1,0:T(8,128)S(1)} %bitcast.243, f32[8,8]{0,1:T(8,128)S(1)} %fusion.11, f32[8,8]{0,1:T(8,128)S(1)} %fusion.9), channel_id=1, replica_groups=mesh['grp'=2,'az'=8,'ax'=2] {'grp','az','ax'}, use_global_device_ids=true, to_apply=%region_0.1 | all-reduce | flops 192 | bytes 1536 | tf_op jit(solution)/shard_map/psum | solution.py:115
  117.8 1.9 fusion.31
  123.1 1.2 fusion.121
  125.9 2.1 copy.208
  128.1 1.9 collective-permute-start.8
  130.9 1.3 collective-permute-start.7
  132.2 2.3 collective-permute-start.6
  134.6 2.4 collective-permute-start.5
  137.0 3.1 %convolution_bitcast_fusion.1 = f32[8,54,512]{2,1,0:T(8,128)} fusion(f32[8,54,512]{2,0,1:T(8,128)S(1)} %bitcast.237, f32[6,6]{1,0:T(8,128)S(1)} %copy-done.16, f32[48,48]{1,0:T(8,128)} %bitcast.240), kind=kOutput, calls=%fused_computation.1 | convolution fusion | flops 143341808 | bytes 1778832 | tf_op jit(solution)/shard_map/rs,vsc->vrc/dot_general | solution.py:49
  140.8 2.3 collective-permute-start.9
  145.1 1.2 custom-call.23
  146.4 1.1 copy.209
  147.5 1.3 copy.207
  149.5 2.5 fusion.22
  153.5 1.8 convolution_bitcast_fusion.11
  155.3 1.8 convolution_bitcast_fusion.9
  157.1 1.8 convolution_bitcast_fusion.7
  159.8 39.2 %all-reduce.2 = (f32[8,8]{0,1:T(8,128)S(1)}, f32[8,8]{0,1:T(8,128)}, f32[8,8]{0,1:T(8,128)}) all-reduce(f32[8,8]{0,1:T(8,128)S(1)} %fusion.7, f32[8,8]{0,1:T(8,128)S(1)} %fusion.5, f32[8,8]{0,1:T(8,128)S(1)} %fusion.3), channel_id=1, replica_groups=mesh['grp'=2,'az'=8,'ax'=2] {'grp','az','ax'}, use_global_device_ids=true, to_apply=%region_6.10 | all-reduce | flops 192 | bytes 1536 | tf_op jit(solution)/shard_map/psum | solution.py:115
  205.9 1.5 fusion.119
  209.3 1.9 convolution_add_fusion.2
  211.2 2.2 copy.239
  213.4 2.0 collective-permute-start.13
  216.4 1.3 collective-permute-start.12
  217.6 2.7 collective-permute-start.11
  220.3 2.1 collective-permute-start.10
  222.4 3.1 %convolution_bitcast_fusion = f32[8,54,512]{2,1,0:T(8,128)} fusion(f32[8,54,512]{2,0,1:T(8,128)S(1)} %bitcast.238, f32[6,6]{1,0:T(8,128)S(1)} %copy-done.16, f32[48,48]{1,0:T(8,128)} %bitcast.241), kind=kOutput, calls=%fused_computation | convolution fusion | flops 143341808 | bytes 1778832 | tf_op jit(solution)/shard_map/rs,vsc->vrc/dot_general | solution.py:49
  226.2 2.2 collective-permute-start.14
  229.5 1.3 copy.238
  231.7 1.8 collective-permute-done.10
  233.6 2.4 fusion.18
  237.5 1.8 convolution_bitcast_fusion.5
  239.6 37.9 %psum.55 = f32[8,8]{0,1:T(8,128)S(1)} all-reduce(f32[8,8]{0,1:T(8,128)S(1)} %fusion.1), channel_id=1, replica_groups=mesh['grp'=2,'az'=8,'ax'=2] {'grp','az','ax'}, use_global_device_ids=true, to_apply=%region_9.13 | all-reduce | flops 64 | bytes 512 | tf_op jit(solution)/shard_map/psum | solution.py:115
  286.0 1.4 copy.252
  (174 shorter events, 49.7 us)
Async XLA Ops:
  0.6 2.5 copy-start.7
  5.1 60.1 %collective-permute-start.3 = (f32[8,54,4,1]{1,0,3,2:T(8,128)}, f32[8,54,4,1]{1,0,3,2:T(8,128)S(1)}, u32[]{:S(2)}, u32[]{:S(2)}) collective-permute-start(f32[8,54,4,1]{1,0,3,2:T(8,128)} %copy.166), channel_id=1, source_target_pairs={{0,1},{2,3},{4,5},{6,7},{8,9},{10,11},{12,13},{14,15},{16,17},{18,... | collective-permute-start | bytes 20744 | tf_op jit(solution)/shard_map/ppermute | solution.py:27
  7.5 10.2 %copy-start = (f32[8,48,4,128]{3,2,1,0:T(4,128)S(1)}, f32[8,48,4,128]{3,2,1,0:T(4,128)}, u32[]{:S(2)}) copy-start(f32[8,48,4,128]{3,2,1,0:T(4,128)} %param.24) | copy-start | bytes 2359300
  7.9 58.7 %collective-permute-start.2 = (f32[8,54,4,1]{1,0,3,2:T(8,128)S(1)}, f32[8,54,4,1]{1,0,3,2:T(8,128)S(1)}, u32[]{:S(2)}, u32[]{:S(2)}) collective-permute-start(f32[8,54,4,1]{1,0,3,2:T(8,128)S(1)} %copy.164), channel_id=1, source_target_pairs={{1,0},{3,2},{5,4},{7,6},{9,8},{11,10},{13,12},{15,14},{17,16},{19,... | collective-permute-start | bytes 20744 | tf_op jit(solution)/shard_map/ppermute | solution.py:28
  9.2 58.7 %collective-permute-start.1 = (f32[8,54,1,128]{3,0,1,2:T(8,128)S(1)}, f32[8,54,1,128]{3,0,1,2:T(8,128)S(1)}, u32[]{:S(2)}, u32[]{:S(2)}) collective-permute-start(f32[8,54,1,128]{3,0,1,2:T(8,128)S(1)} %get-tuple-element.110), channel_id=1, source_target_pairs={{0,2},{2,4},{4,6},{6,8},{8,10},{10,12},{12,14},{14,0},{1,3},{3,5},... | collective-permute-start | bytes 663560 | tf_op jit(solution)/shard_map/ppermute | solution.py:27
  11.6 57.0 %collective-permute-start = (f32[8,54,1,128]{3,0,1,2:T(8,128)S(1)}, f32[8,54,1,128]{3,0,1,2:T(8,128)}, u32[]{:S(2)}, u32[]{:S(2)}) collective-permute-start(f32[8,54,1,128]{3,0,1,2:T(8,128)S(1)} %get-tuple-element.109), channel_id=1, source_target_pairs={{2,0},{4,2},{6,4},{8,6},{10,8},{12,10},{14,12},{0,14},{3,1},{5,3},... | collective-permute-start | bytes 663560 | tf_op jit(solution)/shard_map/ppermute | solution.py:28
  16.1 54.9 %collective-permute-start.4 = (f32[8,2,4,128]{3,0,1,2:T(8,128)}, f32[8,2,4,128]{3,0,1,2:T(8,128)}, u32[]{:S(2)}, u32[]{:S(2)}) collective-permute-start(f32[8,2,4,128]{3,0,1,2:T(8,128)} %pad_maximum_fusion.12), channel_id=1, source_target_pairs={{0,16},{16,0},{1,17},{17,1},{2,18},{18,2},{3,19},{19,3},{4,20},{20... | collective-permute-start | bytes 98312 | tf_op jit(solution)/shard_map/ppermute | solution.py:17
  58.6 2.3 copy-start.9
  60.1 0.7 copy-start.16
  60.9 2.4 copy-start.24
  60.9 2.4 copy-start.13
  60.9 2.4 copy-start.22
  63.3 8.4 %copy-start.17 = (f32[4,128]{1,0:T(4,128)}, f32[4,128]{1,0:T(4,128)S(1)}, u32[]{:S(2)}) copy-start(f32[4,128]{1,0:T(4,128)S(1)} %get-tuple-element.118) | copy-start | bytes 6148
  64.0 4.6 %copy-start.1 = (f32[8,54,512]{2,1,0:T(8,128)S(1)}, f32[8,54,512]{2,1,0:T(8,128)}, u32[]{:S(2)}) copy-start(f32[8,54,512]{2,1,0:T(8,128)} %convolution_bitcast_fusion.2) | copy-start | bytes 2654212
  67.9 0.7 copy-start.10
  75.1 1.8 copy-start.8
  121.2 0.7 copy-start.19
  128.1 18.3 %collective-permute-start.8 = (f32[8,54,4,1]{1,0,3,2:T(8,128)}, f32[8,54,4,1]{1,0,3,2:T(8,128)}, u32[]{:S(2)}, u32[]{:S(2)}) collective-permute-start(f32[8,54,4,1]{1,0,3,2:T(8,128)} %copy.208), channel_id=1, source_target_pairs={{0,1},{2,3},{4,5},{6,7},{8,9},{10,11},{12,13},{14,15},{16,17},{18,... | collective-permute-start | bytes 20744 | tf_op jit(solution)/shard_map/ppermute | solution.py:27
  130.9 16.6 %collective-permute-start.7 = (f32[8,54,4,1]{1,0,3,2:T(8,128)}, f32[8,54,4,1]{1,0,3,2:T(8,128)S(1)}, u32[]{:S(2)}, u32[]{:S(2)}) collective-permute-start(f32[8,54,4,1]{1,0,3,2:T(8,128)} %copy.206), channel_id=1, source_target_pairs={{1,0},{3,2},{5,4},{7,6},{9,8},{11,10},{13,12},{15,14},{17,16},{19,... | collective-permute-start | bytes 20744 | tf_op jit(solution)/shard_map/ppermute | solution.py:28
  132.2 16.6 %collective-permute-start.6 = (f32[8,54,1,128]{3,0,1,2:T(8,128)}, f32[8,54,1,128]{3,0,1,2:T(8,128)S(1)}, u32[]{:S(2)}, u32[]{:S(2)}) collective-permute-start(f32[8,54,1,128]{3,0,1,2:T(8,128)} %get-tuple-element.106), channel_id=1, source_target_pairs={{0,2},{2,4},{4,6},{6,8},{8,10},{10,12},{12,14},{14,0},{1,3},{3,5},... | collective-permute-start | bytes 663560 | tf_op jit(solution)/shard_map/ppermute | solution.py:27
  134.6 15.0 %collective-permute-start.5 = (f32[8,54,1,128]{3,0,1,2:T(8,128)}, f32[8,54,1,128]{3,0,1,2:T(8,128)}, u32[]{:S(2)}, u32[]{:S(2)}) collective-permute-start(f32[8,54,1,128]{3,0,1,2:T(8,128)} %get-tuple-element.105), channel_id=1, source_target_pairs={{2,0},{4,2},{6,4},{8,6},{10,8},{12,10},{14,12},{0,14},{3,1},{5,3},... | collective-permute-start | bytes 663560 | tf_op jit(solution)/shard_map/ppermute | solution.py:28
  137.0 3.1 %copy-start.14 = (f32[8,1,4,128]{3,0,1,2:T(8,128)S(1)}, f32[8,1,4,128]{3,0,1,2:T(8,128)}, u32[]{:S(2)}) copy-start(f32[8,1,4,128]{3,0,1,2:T(8,128)} %get-tuple-element.103) | copy-start | bytes 49156
  137.0 3.1 %copy-start.15 = (f32[8,1,4,128]{3,0,1,2:T(8,128)S(1)}, f32[8,1,4,128]{3,0,1,2:T(8,128)}, u32[]{:S(2)}) copy-start(f32[8,1,4,128]{3,0,1,2:T(8,128)} %get-tuple-element.104) | copy-start | bytes 49156
  140.8 11.2 %collective-permute-start.9 = (f32[8,2,4,128]{3,0,1,2:T(8,128)}, f32[8,2,4,128]{3,0,1,2:T(8,128)}, u32[]{:S(2)}, u32[]{:S(2)}) collective-permute-start(f32[8,2,4,128]{3,0,1,2:T(8,128)} %pad_maximum_fusion.13), channel_id=1, source_target_pairs={{0,16},{16,0},{1,17},{17,1},{2,18},{18,2},{3,19},{19,3},{4,20},{20... | collective-permute-start | bytes 98312 | tf_op jit(solution)/shard_map/ppermute | solution.py:17
  148.8 0.7 copy-start.11
  152.0 0.8 copy-start.18
  202.1 0.9 copy-start.21
  203.0 0.7 copy-start.23
  203.9 0.7 copy-start.20
  208.1 1.2 copy-start.3
  211.2 4.2 %copy-start.2 = (f32[8,54,4,1]{3,0,1,2:T(8,128)S(1)}, f32[8,54,4,1]{3,0,1,2:T(8,128)}, u32[]{:S(2)}) copy-start(f32[8,54,4,1]{3,0,1,2:T(8,128)} %get-tuple-element.101) | copy-start | bytes 20740
  213.4 15.0 %collective-permute-start.13 = (f32[8,54,4,1]{1,0,3,2:T(8,128)}, f32[8,54,4,1]{1,0,3,2:T(8,128)}, u32[]{:S(2)}, u32[]{:S(2)}) collective-permute-start(f32[8,54,4,1]{1,0,3,2:T(8,128)} %copy.239), channel_id=1, source_target_pairs={{0,1},{2,3},{4,5},{6,7},{8,9},{10,11},{12,13},{14,15},{16,17},{18,... | collective-permute-start | bytes 20744 | tf_op jit(solution)/shard_map/ppermute | solution.py:27
  216.4 13.2 %collective-permute-start.12 = (f32[8,54,4,1]{1,0,3,2:T(8,128)}, f32[8,54,4,1]{1,0,3,2:T(8,128)S(1)}, u32[]{:S(2)}, u32[]{:S(2)}) collective-permute-start(f32[8,54,4,1]{1,0,3,2:T(8,128)} %copy.237), channel_id=1, source_target_pairs={{1,0},{3,2},{5,4},{7,6},{9,8},{11,10},{13,12},{15,14},{17,16},{19,... | collective-permute-start | bytes 20744 | tf_op jit(solution)/shard_map/ppermute | solution.py:28
  217.6 13.4 %collective-permute-start.11 = (f32[8,54,1,128]{3,0,1,2:T(8,128)}, f32[8,54,1,128]{3,0,1,2:T(8,128)S(1)}, u32[]{:S(2)}, u32[]{:S(2)}) collective-permute-start(f32[8,54,1,128]{3,0,1,2:T(8,128)} %get-tuple-element.100), channel_id=1, source_target_pairs={{0,2},{2,4},{4,6},{6,8},{8,10},{10,12},{12,14},{14,0},{1,3},{3,5},... | collective-permute-start | bytes 663560 | tf_op jit(solution)/shard_map/ppermute | solution.py:27
  220.3 13.2 %collective-permute-start.10 = (f32[8,54,1,128]{3,0,1,2:T(8,128)}, f32[8,54,1,128]{3,0,1,2:T(8,128)}, u32[]{:S(2)}, u32[]{:S(2)}) collective-permute-start(f32[8,54,1,128]{3,0,1,2:T(8,128)} %get-tuple-element.99), channel_id=1, source_target_pairs={{2,0},{4,2},{6,4},{8,6},{10,8},{12,10},{14,12},{0,14},{3,1},{5,3},... | collective-permute-start | bytes 663560 | tf_op jit(solution)/shard_map/ppermute | solution.py:28
  226.2 9.8 %collective-permute-start.14 = (f32[8,2,4,128]{3,0,1,2:T(8,128)}, f32[8,2,4,128]{3,0,1,2:T(8,128)}, u32[]{:S(2)}, u32[]{:S(2)}) collective-permute-start(f32[8,2,4,128]{3,0,1,2:T(8,128)} %pad_maximum_fusion.14), channel_id=1, source_target_pairs={{0,16},{16,0},{1,17},{17,1},{2,18},{18,2},{3,19},{19,3},{4,20},{20... | collective-permute-start | bytes 98312 | tf_op jit(solution)/shard_map/ppermute | solution.py:17
  231.1 0.7 copy-start.12
  280.6 1.2 copy-start.6
  281.8 1.8 copy-start.4
  282.7 1.0 copy-start.5
  283.7 1.1 slice-start.2
  284.8 1.2 slice-start
  286.0 1.4 slice-start.3
  287.4 0.9 slice-start.1
